TPU v7x, 32 devices: a whole 2x2x4 slice. The times are simulated.
32 devices in a mesh: dp: 8 (over z, core), expert: 4 (over y, x).
Axes of the slice: x: 2, y: 2, z: 4, core: 2. Of those that a mesh axis runs over, the one named last changes fastest.
Arguments:
- tokens: bfloat16 [24576, 768], P(('dp', 'expert')), may hold values from -6 to 6
- cotangent: bfloat16 [24576, 768], P(('dp', 'expert')), may hold values from -6 to 6
- expert_ids: int32 [24576, 2], P(('dp', 'expert')), may hold values from 0 to 15, all different within a row
- route_gates: float32 [24576, 2], P(('dp', 'expert')), may hold values from 0.25 to 1
- slot_order: int32 [32, 1536], P(('dp', 'expert')), may hold values from 0 to 1535, each once within a row
- prefix_len: int32 [32], P(('dp', 'expert')), may hold values from 1 to 767
- attention_gain: float32 [768], replicated, may hold values from 0.1 to 1.9
- qkv_weight: bfloat16 [768, 2304], replicated, may hold values from -0.21875 to 0.21875
- output_weight: bfloat16 [768, 768], replicated, may hold values from -0.875 to 0.875
- feedforward_gain: float32 [768], replicated, may hold values from 0.1 to 1.9
- shared_gate: bfloat16 [768, 2048], replicated, may hold values from -0.21875 to 0.21875
- shared_up: bfloat16 [768, 2048], replicated, may hold values from -0.21875 to 0.21875
- shared_down: bfloat16 [2048, 768], replicated, may hold values from -0.125 to 0.125
- expert_gate: bfloat16 [16, 768, 2048], P('expert'), may hold values from -0.21875 to 0.21875
- expert_up: bfloat16 [16, 768, 2048], P('expert'), may hold values from -0.21875 to 0.21875
- expert_down: bfloat16 [16, 2048, 768], P('expert'), may hold values from -0.125 to 0.125
Outputs:
- block_out: bfloat16 [24576, 768], P(('dp', 'expert'))
- tokens_grad: bfloat16 [24576, 768], P(('dp', 'expert'))
- attention_gain_grad: float32 [768], P('dp')
- qkv_weight_grad: float32 [768, 2304], P('dp')
- output_weight_grad: float32 [768, 768], P('dp')
- feedforward_gain_grad: float32 [768], P('dp')
- shared_gate_grad: float32 [768, 2048], P('dp')
- shared_up_grad: float32 [768, 2048], P('dp')
- shared_down_grad: float32 [2048, 768], P('dp')
- expert_gate_grad: float32 [16, 768, 2048], P('expert', 'dp')
- expert_up_grad: float32 [16, 768, 2048], P('expert', 'dp')
- expert_down_grad: float32 [16, 2048, 768], P('expert', 'dp')
Inputs may be any that keep to these rules, and one draw needn't show every extreme that they name: `expert_ids`: each token names two different experts; every expert is named by some token. `slot_order`: each row is a permutation of its sequence's pair numbers 2 p + k.
All inputs are finite; a program needn't handle non-finite values.
Results may differ from a plain program's by a relative error of at most 0.023.
Values may be sent and summed in bfloat16 or wider, within the bound.
A program may use at most 320 MiB of HBM per device.

v0:
```python
import jax
import jax.numpy as jnp
from jax import lax
from jax.sharding import PartitionSpec as P

HEADS = 12
HEAD_DIM = 64
E = 16
CAP = 120
epsilon = 1e-06


def rms_forward(values, gain_vector):
    inverse = lax.rsqrt(jnp.mean(values * values, axis=-1, keepdims=True) + epsilon)
    normed = values * inverse
    return (normed * gain_vector, normed, inverse)


def rms_backward(upstream, gain_vector, normed, inverse):
    scaled = upstream * gain_vector
    gain_grad = jnp.sum(upstream * normed, axis=0)
    row_inner = jnp.mean(scaled * normed, axis=-1, keepdims=True)
    return (inverse * (scaled - normed * row_inner), gain_grad)


def rope_tables(length, head_size):
    positions = jnp.arange(length, dtype=jnp.float32)
    frequency = 10000.0 ** (-jnp.arange(head_size // 2, dtype=jnp.float32) * 2.0 / head_size)
    angles = positions[:, None] * frequency[None, :]
    return (jnp.cos(angles)[:, None, :], jnp.sin(angles)[:, None, :])


def rotate(values, cosine, sine_table):
    half_size = values.shape[-1] // 2
    first_half = values[..., :half_size]
    second = values[..., half_size:]
    return jnp.concatenate(
        [first_half * cosine - second * sine_table, second * cosine + first_half * sine_table],
        axis=-1,
    )


def contract_rows(left_side, right_side):
    return lax.dot_general(
        left_side, right_side, (((0,), (0,)), ((), ())), preferred_element_type=jnp.float32
    )


def contract_last(left_side, right_side):
    return lax.dot_general(
        left_side, right_side, (((1,), (1,)), ((), ())), preferred_element_type=jnp.float32
    )


def silu_slope(pre_values):
    sigmoid_gate = jax.nn.sigmoid(pre_values)
    return sigmoid_gate * (1.0 + pre_values * (1.0 - sigmoid_gate))


def shards(
    tokens,
    cotangent,
    expert_ids,
    route_gates,
    slot_order,
    prefix_len,
    attention_gain,
    qkv_weight,
    output_weight,
    feedforward_gain,
    shared_gate,
    shared_up,
    shared_down,
    expert_gate,
    expert_up,
    expert_down,
):
    length, features = tokens.shape
    local_experts = expert_gate.shape[0]
    groups = lax.axis_size("expert")
    pair_count = 2 * length
    score_scale = HEAD_DIM ** (-0.5)
    pair_expert = expert_ids.reshape(pair_count)
    order_row = slot_order[0]
    sorted_expert = pair_expert[order_row]
    onehot = (sorted_expert[:, None] == jnp.arange(E, dtype=jnp.int32)[None, :]).astype(jnp.int32)
    before = jnp.cumsum(onehot, axis=0) - onehot
    sorted_slot = jnp.sum(before * onehot, axis=1)
    position = jnp.zeros((pair_count,), jnp.int32).at[order_row].set(sorted_slot)
    slot_index = jnp.where(position < CAP, pair_expert * CAP + position, E * CAP)
    pair_table = (
        jnp.full((E * CAP + 1,), pair_count, jnp.int32)
        .at[slot_index]
        .set(jnp.arange(pair_count, dtype=jnp.int32))[: E * CAP]
    )
    token_table = pair_table // 2
    zero_row = jnp.zeros((1, features), jnp.bfloat16)
    resid = tokens.astype(jnp.float32)
    normed_one, unit_one, inverse_one = rms_forward(resid, attention_gain)
    normed_low = normed_one.astype(jnp.bfloat16)
    projected = jnp.dot(normed_low, qkv_weight, preferred_element_type=jnp.float32).reshape(
        length, 3, HEADS, HEAD_DIM
    )
    cosine, sine_table = rope_tables(length, HEAD_DIM)
    queries = rotate(projected[:, 0], cosine, sine_table).astype(jnp.bfloat16)
    key_rows = rotate(projected[:, 1], cosine, sine_table).astype(jnp.bfloat16)
    values = projected[:, 2].astype(jnp.bfloat16)
    row_ids = jnp.arange(length)[:, None]
    col_ids = jnp.arange(length)[None, :]
    visible = ((col_ids <= row_ids) | (col_ids < prefix_len[0]))[None]
    scores = (
        jnp.einsum("qhd,khd->hqk", queries, key_rows, preferred_element_type=jnp.float32)
        * score_scale
    )
    scores = jnp.where(visible, scores, -1e30)
    row_peak = jnp.max(scores, axis=-1, keepdims=True)
    exp_scores = jnp.exp(scores - row_peak)
    row_total = jnp.sum(exp_scores, axis=-1, keepdims=True)
    log_total = row_peak + jnp.log(row_total)
    soft_probs = (exp_scores / row_total).astype(jnp.bfloat16)
    attended = jnp.einsum("hqk,khd->qhd", soft_probs, values, preferred_element_type=jnp.float32)
    attended_low = attended.reshape(length, features).astype(jnp.bfloat16)
    attn_branch = jnp.dot(attended_low, output_weight, preferred_element_type=jnp.float32)
    state = resid + attn_branch
    normed_two, unit_two, inverse_two = rms_forward(state, feedforward_gain)
    normed_two_low = normed_two.astype(jnp.bfloat16)
    gate_pre = jnp.dot(normed_two_low, shared_gate, preferred_element_type=jnp.float32)
    up_pre = jnp.dot(normed_two_low, shared_up, preferred_element_type=jnp.float32)
    shared_hidden = (jax.nn.silu(gate_pre) * up_pre).astype(jnp.bfloat16)
    shared_branch = jnp.dot(shared_hidden, shared_down, preferred_element_type=jnp.float32)
    padded_rows = jnp.concatenate([normed_two_low, zero_row], axis=0)
    outgoing = padded_rows[token_table].reshape(groups, local_experts, CAP, features)
    arrived = lax.all_to_all(outgoing, "expert", split_axis=0, concat_axis=0, tiled=True)
    expert_gate_pre = jnp.einsum(
        "slcd,ldf->slcf", arrived, expert_gate, preferred_element_type=jnp.float32
    )
    expert_up_pre = jnp.einsum(
        "slcd,ldf->slcf", arrived, expert_up, preferred_element_type=jnp.float32
    )
    expert_hidden = (jax.nn.silu(expert_gate_pre) * expert_up_pre).astype(jnp.bfloat16)
    expert_result = jnp.einsum(
        "slcf,lfd->slcd", expert_hidden, expert_down, preferred_element_type=jnp.float32
    ).astype(jnp.bfloat16)
    returned = lax.all_to_all(expert_result, "expert", split_axis=0, concat_axis=0, tiled=True)
    returned_pad = jnp.concatenate([returned.reshape(E * CAP, features), zero_row], axis=0)
    picked = returned_pad[slot_index].astype(jnp.float32).reshape(length, 2, features)
    mixture = jnp.sum(picked * route_gates[:, :, None], axis=1)
    block_out = (state + shared_branch + mixture).astype(jnp.bfloat16)
    upstream = cotangent.astype(jnp.float32)
    pair_grad = (route_gates[:, :, None] * upstream[:, None, :]).reshape(pair_count, features)
    pair_grad_pad = jnp.concatenate([pair_grad, jnp.zeros((1, features), jnp.float32)], axis=0)
    slot_grad = (
        pair_grad_pad[pair_table].astype(jnp.bfloat16).reshape(groups, local_experts, CAP, features)
    )
    slot_grad_in = lax.all_to_all(slot_grad, "expert", split_axis=0, concat_axis=0, tiled=True)
    down_w_grad = jnp.einsum(
        "slcf,slcd->lfd", expert_hidden, slot_grad_in, preferred_element_type=jnp.float32
    )
    expert_hidden_grad = jnp.einsum(
        "slcd,lfd->slcf", slot_grad_in, expert_down, preferred_element_type=jnp.float32
    )
    expert_gate_back = (expert_hidden_grad * expert_up_pre * silu_slope(expert_gate_pre)).astype(
        jnp.bfloat16
    )
    expert_up_back = (expert_hidden_grad * jax.nn.silu(expert_gate_pre)).astype(jnp.bfloat16)
    gate_w_grad = jnp.einsum(
        "slcd,slcf->ldf", arrived, expert_gate_back, preferred_element_type=jnp.float32
    )
    up_w_grad = jnp.einsum(
        "slcd,slcf->ldf", arrived, expert_up_back, preferred_element_type=jnp.float32
    )
    dispatched_grad = jnp.einsum(
        "slcf,ldf->slcd", expert_gate_back, expert_gate, preferred_element_type=jnp.float32
    )
    dispatched_grad = dispatched_grad + jnp.einsum(
        "slcf,ldf->slcd", expert_up_back, expert_up, preferred_element_type=jnp.float32
    )
    sent_back = lax.all_to_all(
        dispatched_grad.astype(jnp.bfloat16), "expert", split_axis=0, concat_axis=0, tiled=True
    )
    expert_sums = (
        lax.psum_scatter(
            gate_w_grad.astype(jnp.bfloat16), "dp", scatter_dimension=1, tiled=True
        ).astype(jnp.float32),
        lax.psum_scatter(
            up_w_grad.astype(jnp.bfloat16), "dp", scatter_dimension=1, tiled=True
        ).astype(jnp.float32),
        lax.psum_scatter(
            down_w_grad.astype(jnp.bfloat16), "dp", scatter_dimension=1, tiled=True
        ).astype(jnp.float32),
    )
    back_pad = jnp.concatenate([sent_back.reshape(E * CAP, features), zero_row], axis=0)
    from_experts = jnp.sum(
        back_pad[slot_index].astype(jnp.float32).reshape(length, 2, features), axis=1
    )
    shared_down_grad = contract_rows(shared_hidden, cotangent)
    shared_hidden_grad = contract_last(cotangent, shared_down)
    gate_back = (shared_hidden_grad * up_pre * silu_slope(gate_pre)).astype(jnp.bfloat16)
    up_back = (shared_hidden_grad * jax.nn.silu(gate_pre)).astype(jnp.bfloat16)
    shared_gate_grad = contract_rows(normed_two_low, gate_back)
    shared_up_grad = contract_rows(normed_two_low, up_back)
    normed_two_grad = (
        contract_last(gate_back, shared_gate) + contract_last(up_back, shared_up) + from_experts
    )
    state_norm_grad, feedforward_gain_grad = rms_backward(
        normed_two_grad, feedforward_gain, unit_two, inverse_two
    )
    state_grad = upstream + state_norm_grad
    branch_grad = state_grad.astype(jnp.bfloat16)
    output_weight_grad = contract_rows(attended_low, branch_grad)
    attended_grad = (
        contract_last(branch_grad, output_weight)
        .astype(jnp.bfloat16)
        .reshape(length, HEADS, HEAD_DIM)
    )
    scores_again = (
        jnp.einsum("qhd,khd->hqk", queries, key_rows, preferred_element_type=jnp.float32)
        * score_scale
    )
    probs_again = jnp.exp(jnp.where(visible, scores_again, -1e30) - log_total)
    values_grad = jnp.einsum(
        "hqk,qhd->khd",
        probs_again.astype(jnp.bfloat16),
        attended_grad,
        preferred_element_type=jnp.float32,
    )
    prob_grad = jnp.einsum(
        "qhd,khd->hqk", attended_grad, values, preferred_element_type=jnp.float32
    )
    row_inner = jnp.sum(prob_grad * probs_again, axis=-1, keepdims=True)
    score_grad = (probs_again * (prob_grad - row_inner)).astype(jnp.bfloat16)
    queries_grad = (
        jnp.einsum("hqk,khd->qhd", score_grad, key_rows, preferred_element_type=jnp.float32)
        * score_scale
    )
    keys_grad = (
        jnp.einsum("hqk,qhd->khd", score_grad, queries, preferred_element_type=jnp.float32)
        * score_scale
    )
    queries_grad = rotate(queries_grad, cosine, -sine_table)
    keys_grad = rotate(keys_grad, cosine, -sine_table)
    projected_grad = (
        jnp.stack([queries_grad, keys_grad, values_grad], axis=1)
        .reshape(length, 3 * features)
        .astype(jnp.bfloat16)
    )
    qkv_weight_grad = contract_rows(normed_low, projected_grad)
    normed_one_grad = contract_last(projected_grad, qkv_weight)
    tokens_norm_grad, attention_gain_grad = rms_backward(
        normed_one_grad, attention_gain, unit_one, inverse_one
    )
    tokens_grad = (state_grad + tokens_norm_grad).astype(jnp.bfloat16)
    partial_sums = (
        lax.psum_scatter(
            attention_gain_grad.astype(jnp.bfloat16), "dp", scatter_dimension=0, tiled=True
        ).astype(jnp.float32),
        lax.psum_scatter(
            qkv_weight_grad.astype(jnp.bfloat16), "dp", scatter_dimension=0, tiled=True
        ).astype(jnp.float32),
        lax.psum_scatter(
            output_weight_grad.astype(jnp.bfloat16), "dp", scatter_dimension=0, tiled=True
        ).astype(jnp.float32),
        lax.psum_scatter(
            feedforward_gain_grad.astype(jnp.bfloat16), "dp", scatter_dimension=0, tiled=True
        ).astype(jnp.float32),
        lax.psum_scatter(
            shared_gate_grad.astype(jnp.bfloat16), "dp", scatter_dimension=0, tiled=True
        ).astype(jnp.float32),
        lax.psum_scatter(
            shared_up_grad.astype(jnp.bfloat16), "dp", scatter_dimension=0, tiled=True
        ).astype(jnp.float32),
        lax.psum_scatter(
            shared_down_grad.astype(jnp.bfloat16), "dp", scatter_dimension=0, tiled=True
        ).astype(jnp.float32),
    )
    dense_sums = (
        lax.psum(partial_sums[0].astype(jnp.bfloat16), "expert").astype(jnp.float32),
        lax.psum(partial_sums[1].astype(jnp.bfloat16), "expert").astype(jnp.float32),
        lax.psum(partial_sums[2].astype(jnp.bfloat16), "expert").astype(jnp.float32),
        lax.psum(partial_sums[3].astype(jnp.bfloat16), "expert").astype(jnp.float32),
        lax.psum(partial_sums[4].astype(jnp.bfloat16), "expert").astype(jnp.float32),
        lax.psum(partial_sums[5].astype(jnp.bfloat16), "expert").astype(jnp.float32),
        lax.psum(partial_sums[6].astype(jnp.bfloat16), "expert").astype(jnp.float32),
    )
    return (
        block_out,
        tokens_grad,
        dense_sums[0],
        dense_sums[1],
        dense_sums[2],
        dense_sums[3],
        dense_sums[4],
        dense_sums[5],
        dense_sums[6],
        expert_sums[0],
        expert_sums[1],
        expert_sums[2],
    )


def solution(mesh):
    return jax.shard_map(
        shards,
        mesh=mesh,
        in_specs=(
            P(("dp", "expert"), None),
            P(("dp", "expert"), None),
            P(("dp", "expert"), None),
            P(("dp", "expert"), None),
            P(("dp", "expert"), None),
            P(("dp", "expert")),
            P(),
            P(),
            P(),
            P(),
            P(),
            P(),
            P(),
            P("expert", None, None),
            P("expert", None, None),
            P("expert", None, None),
        ),
        out_specs=(
            P(("dp", "expert"), None),
            P(("dp", "expert"), None),
            P("dp"),
            P("dp", None),
            P("dp", None),
            P("dp"),
            P("dp", None),
            P("dp", None),
            P("dp", None),
            P("expert", "dp", None),
            P("expert", "dp", None),
            P("expert", "dp", None),
        ),
        check_vma=False,
    )
```

profile of v0, /device:TPU:0, one launch (start us, length us, event | category | flops | bytes accessed | tf_op | source)
XLA Modules:
  0.0 993.0 jit_solution(16320943424098945938)
XLA Ops:
  16.8 12.1 %fusion.85 = (f32[12,768]{1,0:T(8,128)S(1)}, f32[12,768,768]{1,2,0:T(8,128)}) fusion(bf16[768,12,32]{0,2,1:T(8,128)(2,1)S(1)} %get-tuple-element.43, bf16[768,12,32]{0,2,1:T(8,128)(2,1)S(1)} %get-tuple-element.44, bf16[768,12,32]{0,2,1:T(8,128)(2,1)S(1)} %get-tuple-element.38, bf16[768,12,32]{0,2,1:T(8,128)(2,1)S(1)} %get-tuple-element.37, ...), kind=kOutput, calls=%fused_computation.163 | convolution fusion | flops 931912704 | bytes 31297536 | tf_op jit(solution)/shard_map/qhd,khd->hqk/dot_general | solution.py:112
  28.9 11.6 %fusion = f32[12,768]{1,0:T(8,128)S(1)} fusion(f32[12,768,768]{1,2,0:T(8,128)} %get-tuple-element.51, f32[12,768]{1,0:T(8,128)S(1)} %get-tuple-element.50), kind=kLoop, calls=%fused_computation.16 | loop fusion | flops 14146560 | bytes 28385280 | tf_op jit(solution)/shard_map/reduce_sum | solution.py:118
  40.5 12.8 %fusion.55 = bf16[12,64,768]{2,1,0:T(8,128)(2,1)} fusion(f32[12,768,768]{1,2,0:T(8,128)} %get-tuple-element.51, f32[12,768]{1,0:T(8,128)S(1)} %fusion, f32[12,768]{1,0:T(8,128)S(1)} %get-tuple-element.50, f32[768,3,12,64]{0,3,2,1:T(8,128)S(1)} %bitcast.173), kind=kOutput, calls=%fused_computation.101 | convolution fusion | flops 927793152 | bytes 30769152 | tf_op jit(solution)/shard_map/hqk,khd->qhd/dot_general | solution.py:121
  91.2 9.4 reduce-window.6
  122.6 9.9 gather_fusion.1
  163.1 10.5 %gather_fusion.3 = bf16[1920,768]{1,0:T(8,128)(2,1)} fusion(bf16[1537,768]{1,0:T(8,128)(2,1)} %concatenate.32, s32[2048]{0:T(1024)S(1)} %get-tuple-element.58), kind=kCustom, calls=%fused_computation.3 | custom fusion | bytes 5905920 | tf_op jit(solution)/shard_map/gather | solution.py:153
  178.5 14.8 %fusion.17 = f32[4,4,120,2048]{3,2,1,0:T(8,128)} fusion(bf16[4,768,2048]{2,1,0:T(8,128)(2,1)} %param.30, bf16[4,4,120,768]{3,2,1,0:T(8,128)(2,1)} %all-to-all-done), kind=kOutput, calls=%fused_computation.38 | convolution fusion | flops 6039797760 | bytes 31260672 | tf_op jit(solution)/shard_map/slcd,ldf->slcf/dot_general | solution.py:137
  193.3 14.7 %fusion.21 = f32[4,4,120,2048]{3,2,1,0:T(8,128)} fusion(bf16[4,768,2048]{2,1,0:T(8,128)(2,1)} %param.29, bf16[4,4,120,768]{3,2,1,0:T(8,128)(2,1)} %all-to-all-done), kind=kOutput, calls=%fused_computation.42 | convolution fusion | flops 6039797760 | bytes 31260672 | tf_op jit(solution)/shard_map/slcd,ldf->slcf/dot_general | solution.py:134
  213.6 25.5 %fusion.3 = (bf16[4,4,120,2048]{3,2,0,1:T(8,128)(2,1)}, bf16[4,4,120,2048]{3,2,0,1:T(8,128)(2,1)}, bf16[4,4,120,2048]{3,2,0,1:T(8,128)(2,1)}) fusion(f32[4,4,120,2048]{3,2,1,0:T(8,128)} %fusion.17, f32[4,4,120,2048]{3,2,1,0:T(8,128)} %fusion.21, bf16[4,2048,768]{2,1,0:T(8,128)(2,1)} %param.31, bf16[4,4,120,768]{3,2,1,0:T(8,128)(2,1)} %all-to-all-done.2), kind=kOutput, calls=%fused_computation.21 | convolution fusion | flops 6098780160 | bytes 70582272 | tf_op jit(solution)/shard_map/slcd,lfd->slcf/dot_general | solution.py:159
  239.1 14.3 %fusion.15 = f32[4,4,120,768]{3,2,1,0:T(8,128)} fusion(bf16[4,4,120,2048]{3,2,0,1:T(8,128)(2,1)} %get-tuple-element.27, bf16[4,768,2048]{2,1,0:T(8,128)(2,1)} %param.30), kind=kOutput, calls=%fused_computation.36 | convolution fusion | flops 6039797760 | bytes 26345472 | tf_op jit(solution)/shard_map/slcf,ldf->slcd/dot_general | solution.py:175
  253.4 15.1 %fusion.34 = bf16[4,4,120,768]{3,2,0,1:T(8,128)(2,1)} fusion(f32[4,4,120,768]{3,2,1,0:T(8,128)} %fusion.15, bf16[4,4,120,2048]{3,2,0,1:T(8,128)(2,1)} %get-tuple-element.25, bf16[4,768,2048]{2,1,0:T(8,128)(2,1)} %param.29), kind=kOutput, calls=%fused_computation.69 | convolution fusion | flops 6042746880 | bytes 29294592 | tf_op jit(solution)/shard_map/slcf,ldf->slcd/dot_general | solution.py:172
  292.4 18.2 %all-to-all-done.3 = bf16[4,4,120,768]{3,2,1,0:T(8,128)(2,1)} async-done(((bf16[4,4,120,768]{3,2,1,0:T(8,128)(2,1)}), bf16[4,4,120,768]{3,2,1,0:T(8,128)(2,1)}, u32[]{:S(2)}, u32[]{:S(2)}) %all-to-all-start.3) | async-done | bytes 2949152 | tf_op jit(solution)/shard_map/all_to_all | solution.py:178
  314.3 8.9 gather_fusion.4
  329.7 9.4 reduce_sum.104
  355.0 23.3 %multiply_reduce_fusion = (f32[12,768]{1,0:T(8,128)}, f32[12,768,768]{1,2,0:T(8,128)}) fusion(f32[12,768,768]{1,2,0:T(8,128)} %get-tuple-element.51, f32[12,768]{1,0:T(8,128)S(1)} %copy-done.20, bf16[768,12,64]{0,2,1:T(8,128)(2,1)S(1)} %bitcast.175, f32[768,3,12,64]{0,3,2,1:T(8,128)} %bitcast.174), kind=kOutput, calls=%fused_computation.8 | convolution fusion | flops 927194112 | bytes 59056128 | tf_op jit(solution)/shard_map/qhd,khd->hqk/dot_general | solution.py:227
  378.3 23.3 %multiply_convert_fusion = bf16[12,768,768]{1,2,0:T(8,128)(2,1)} fusion(f32[12,768,768]{1,2,0:T(8,128)} %get-tuple-element.56, f32[12,768,768]{1,2,0:T(8,128)} %get-tuple-element.51, f32[12,768]{1,0:T(8,128)} %get-tuple-element.55, f32[12,768]{1,0:T(8,128)} %log_add_fusion), kind=kLoop, calls=%fused_computation.7 | loop fusion | flops 28311552 | bytes 70852608 | tf_op jit(solution)/shard_map/convert_element_type | solution.py:231
  401.6 11.2 %multiply_bitcast_fusion = f32[768,12,64]{0,2,1:T(8,128)} fusion(bf16[12,768,768]{1,2,0:T(8,128)(2,1)} %multiply_convert_fusion, bf16[768,12,32]{0,2,1:T(8,128)(2,1)} %copy-done.18, bf16[768,12,32]{0,2,1:T(8,128)(2,1)} %copy-done.17), kind=kOutput, calls=%fused_computation.87 | convolution fusion | flops 908918784 | bytes 17694720 | tf_op jit(solution)/shard_map/hqk,qhd->khd/dot_general | solution.py:237
  412.9 9.0 multiply_bitcast_fusion.1
  426.3 11.7 %fusion.56 = bf16[768,1,12,64]{0,3,2,1:T(8,128)(2,1)S(1)} fusion(bf16[768,12,64]{0,2,1:T(8,128)(2,1)S(1)} %bitcast.176, f32[12,768,768]{1,2,0:T(8,128)} %get-tuple-element.51, f32[12,768]{1,0:T(8,128)S(1)} %copy-done.21), kind=kOutput, calls=%fused_computation.102 | convolution fusion | flops 920715264 | bytes 30707712 | tf_op jit(solution)/shard_map/hqk,qhd->khd/dot_general | solution.py:221
  445.3 9.8 reduce-scatter.11.cloned.1.call-done
  455.1 44.2 %reduce-scatter.9.cloned.1.call-done = bf16[96,2304]{1,0:T(8,128)(2,1)} async-done(((bf16[768,2304]{1,0:T(8,128)(2,1)}), bf16[96,2304]{1,0:T(8,128)(2,1)}) %reduce-scatter.9.cloned.1.call-update) | async-done | bytes 442384 | tf_op jit(solution)/shard_map/reduce_scatter | solution.py:257
  499.4 13.0 %bitcast_convert_fusion = bf16[4,2048,768]{2,1,0:T(8,128)(2,1)} fusion(bf16[4,4,120,2048]{3,2,0,1:T(8,128)(2,1)} %get-tuple-element.26, bf16[4,4,120,768]{3,2,1,0:T(8,128)(2,1)} %all-to-all-done.2), kind=kOutput, calls=%fused_computation.13 | convolution fusion | flops 6046089216 | bytes 23396352 | tf_op jit(solution)/shard_map/slcf,slcd->lfd/dot_general | solution.py:156
  512.4 12.7 %bitcast_convert_fusion.2 = bf16[4,768,2048]{2,1,0:T(8,128)(2,1)} fusion(bf16[4,4,120,768]{3,2,1,0:T(8,128)(2,1)} %all-to-all-done, bf16[4,4,120,2048]{3,2,0,1:T(8,128)(2,1)} %get-tuple-element.25), kind=kOutput, calls=%fused_computation.15 | convolution fusion | flops 6046089216 | bytes 23396352 | tf_op jit(solution)/shard_map/slcd,slcf->ldf/dot_general | solution.py:166
  525.2 13.2 %bitcast_convert_fusion.1 = bf16[4,768,2048]{2,1,0:T(8,128)(2,1)} fusion(bf16[4,4,120,768]{3,2,1,0:T(8,128)(2,1)} %all-to-all-done, bf16[4,4,120,2048]{3,2,0,1:T(8,128)(2,1)} %get-tuple-element.27), kind=kOutput, calls=%fused_computation.14 | convolution fusion | flops 6046089216 | bytes 23396352 | tf_op jit(solution)/shard_map/slcd,slcf->ldf/dot_general | solution.py:169
  538.5 12.7 %convert_bitcast_fusion = bf16[4,4,120,768]{3,2,0,1:T(8,128)(2,1)S(1)} fusion(bf16[4,4,120,2048]{3,2,0,1:T(8,128)(2,1)} %get-tuple-element.26, bf16[4,2048,768]{2,1,0:T(8,128)(2,1)} %param.31), kind=kOutput, calls=%fused_computation.70 | convolution fusion | flops 6041272320 | bytes 23396352 | tf_op jit(solution)/shard_map/slcf,lfd->slcd/dot_general | solution.py:141
  559.7 38.6 %all-to-all-done.1 = bf16[4,4,120,768]{3,2,1,0:T(8,128)(2,1)} async-done(((bf16[4,4,120,768]{3,2,1,0:T(8,128)(2,1)}), bf16[4,4,120,768]{3,2,1,0:T(8,128)(2,1)}, u32[]{:S(2)}, u32[]{:S(2)}) %all-to-all-start.1) | async-done | bytes 2949152 | tf_op jit(solution)/shard_map/all_to_all | solution.py:144
  625.6 18.0 %all-reduce.6 = (bf16[768]{0:T(1024)(128)(2,1)}, bf16[768]{0:T(1024)(128)(2,1)}) all-reduce(bf16[768]{0:T(1024)(128)(2,1)} %get-tuple-element.14, bf16[768]{0:T(1024)(128)(2,1)S(1)} %copy-done.39), channel_id=2, replica_groups=mesh['dp'=8,'expert'=4] {'dp'}, use_global_device_ids=true, to_apply=%region_15.16.clone | all-reduce | flops 1536 | bytes 6144
  645.6 9.7 all-reduce.7
  662.2 9.7 multiply_reduce_fusion.1
  687.3 35.5 %reduce-scatter.23.cloned.1.call-done = bf16[4,256,768]{2,1,0:T(8,128)(2,1)} async-done(((bf16[4,2048,768]{2,1,0:T(8,128)(2,1)}), bf16[4,256,768]{2,1,0:T(8,128)(2,1)}) %reduce-scatter.23.cloned.1.call-update) | async-done | bytes 1572880 | tf_op jit(solution)/shard_map/reduce_scatter | solution.py:188
  726.1 126.7 %reduce-scatter.19.cloned.1.call-done = bf16[4,96,2048]{2,1,0:T(8,128)(2,1)} async-done(((bf16[4,768,2048]{2,1,0:T(8,128)(2,1)}), bf16[4,96,2048]{2,1,0:T(8,128)(2,1)}) %reduce-scatter.19.cloned.1.call-update) | async-done | bytes 1572880 | tf_op jit(solution)/shard_map/reduce_scatter | solution.py:182
  856.2 126.6 %reduce-scatter.21.cloned.1.call-done = bf16[4,96,2048]{2,1,0:T(8,128)(2,1)} async-done(((bf16[4,768,2048]{2,1,0:T(8,128)(2,1)}), bf16[4,96,2048]{2,1,0:T(8,128)(2,1)}) %reduce-scatter.21.cloned.1.call-update) | async-done | bytes 1572880 | tf_op jit(solution)/shard_map/reduce_scatter | solution.py:185
  (196 shorter events, 240.7 us)
Async XLA Ops:
  7.2 438.0 %reduce-scatter.13.cloned.1.call-start = ((), (), s32[]{:S(2)}) async-start(), calls=%async_computation.14 | async-start | bytes 3538944 | tf_op jit(solution)/shard_map/reduce_scatter | solution.py:266
  15.5 25.0 %copy-start.4 = (f32[768,2304]{0,1:T(8,128)}, f32[768,2304]{0,1:T(8,128)S(1)}, u32[]{:S(2)}) copy-start(f32[768,2304]{0,1:T(8,128)S(1)} %fusion.66) | copy-start | bytes 21233668
  16.7 12.1 %copy-start.13 = (bf16[768,12,32]{0,2,1:T(8,128)(2,1)}, bf16[768,12,32]{0,2,1:T(8,128)(2,1)S(1)}, u32[]{:S(2)}) copy-start(bf16[768,12,32]{0,2,1:T(8,128)(2,1)S(1)} %get-tuple-element.43) | copy-start | bytes 1769476
  16.7 12.1 %copy-start.15 = (bf16[768,12,32]{0,2,1:T(8,128)(2,1)}, bf16[768,12,32]{0,2,1:T(8,128)(2,1)S(1)}, u32[]{:S(2)}) copy-start(bf16[768,12,32]{0,2,1:T(8,128)(2,1)S(1)} %get-tuple-element.44) | copy-start | bytes 1769476
  16.8 12.1 %copy-start.17 = (bf16[768,12,32]{0,2,1:T(8,128)(2,1)}, bf16[768,12,32]{0,2,1:T(8,128)(2,1)S(1)}, u32[]{:S(2)}) copy-start(bf16[768,12,32]{0,2,1:T(8,128)(2,1)S(1)} %get-tuple-element.37) | copy-start | bytes 1769476
  16.8 12.1 %copy-start.18 = (bf16[768,12,32]{0,2,1:T(8,128)(2,1)}, bf16[768,12,32]{0,2,1:T(8,128)(2,1)S(1)}, u32[]{:S(2)}) copy-start(bf16[768,12,32]{0,2,1:T(8,128)(2,1)S(1)} %get-tuple-element.38) | copy-start | bytes 1769476
  28.9 11.6 %copy-start.24 = (f32[12,768]{1,0:T(8,128)}, f32[12,768]{1,0:T(8,128)S(1)}, u32[]{:S(2)}) copy-start(f32[12,768]{1,0:T(8,128)S(1)} %get-tuple-element.50) | copy-start | bytes 110596
  40.5 12.9 %copy-start.25 = (f32[12,768]{1,0:T(8,128)}, f32[12,768]{1,0:T(8,128)S(1)}, u32[]{:S(2)}) copy-start(f32[12,768]{1,0:T(8,128)S(1)} %fusion) | copy-start | bytes 110596
  40.5 12.9 %copy-start.8 = (bf16[768,768]{1,0:T(8,128)(2,1)S(1)}, bf16[768,768]{1,0:T(8,128)(2,1)}, u32[]{:S(2)}) copy-start(bf16[768,768]{1,0:T(8,128)(2,1)} %param.16) | copy-start | bytes 3538948
  40.5 12.9 %copy-start.43 = (bf16[768,768]{1,0:T(8,128)(2,1)S(1)}, bf16[768,768]{1,0:T(8,128)(2,1)}, u32[]{:S(2)}) copy-start(bf16[768,768]{1,0:T(8,128)(2,1)} %param.24) | copy-start | bytes 3538948
  58.7 13.1 %copy-start.7 = (bf16[768,768]{1,0:T(8,128)(2,1)}, bf16[768,768]{1,0:T(8,128)(2,1)S(1)}, u32[]{:S(2)}) copy-start(bf16[768,768]{1,0:T(8,128)(2,1)S(1)} %multiply_convert_fusion.4) | copy-start | bytes 3538948
  115.6 7.0 copy-start.28
  132.5 41.1 %all-to-all-start = ((bf16[4,4,120,768]{3,2,1,0:T(8,128)(2,1)}), bf16[4,4,120,768]{3,2,1,0:T(8,128)(2,1)}, u32[]{:S(2)}, u32[]{:S(2)}) async-start(bf16[4,4,120,768]{3,2,1,0:T(8,128)(2,1)} %bitcast.170), calls=%async_computation | async-start | bytes 5898240 | tf_op jit(solution)/shard_map/all_to_all | solution.py:133
  137.6 307.6 %reduce-scatter.15.cloned.1.call-start = ((), (), s32[]{:S(2)}) async-start(), calls=%async_computation.15 | async-start | bytes 3538944 | tf_op jit(solution)/shard_map/reduce_scatter | solution.py:269
  173.6 40.1 %all-to-all-start.2 = ((bf16[4,4,120,768]{3,2,1,0:T(8,128)(2,1)}), bf16[4,4,120,768]{3,2,1,0:T(8,128)(2,1)}, u32[]{:S(2)}, u32[]{:S(2)}) async-start(bf16[4,4,120,768]{3,2,1,0:T(8,128)(2,1)} %bitcast.171), calls=%async_computation.2 | async-start | bytes 5898240 | tf_op jit(solution)/shard_map/all_to_all | solution.py:155
  272.2 38.5 %all-to-all-start.3 = ((bf16[4,4,120,768]{3,2,1,0:T(8,128)(2,1)}), bf16[4,4,120,768]{3,2,1,0:T(8,128)(2,1)}, u32[]{:S(2)}, u32[]{:S(2)}) async-start(bf16[4,4,120,768]{3,2,1,0:T(8,128)(2,1)} %copy.57), calls=%async_computation.3 | async-start | bytes 5898240 | tf_op jit(solution)/shard_map/all_to_all | solution.py:178
  276.8 168.5 %reduce-scatter.17.cloned.1.call-start = ((), (), s32[]{:S(2)}) async-start(), calls=%async_computation.16 | async-start | bytes 3538944 | tf_op jit(solution)/shard_map/reduce_scatter | solution.py:272
  283.4 171.7 %reduce-scatter.11.cloned.1.call-start = ((), (), s32[]{:S(2)}) async-start(), calls=%async_computation.13 | async-start | bytes 1327104 | tf_op jit(solution)/shard_map/reduce_scatter | solution.py:260
  329.6 9.4 copy-start.27
  329.7 9.4 copy-start.32
  339.0 8.6 copy-start.2
  339.0 8.6 copy-start.6
  355.0 23.3 %copy-start.10 = (bf16[768,768]{0,1:T(8,128)(2,1)}, bf16[768,768]{0,1:T(8,128)(2,1)S(1)}, u32[]{:S(2)}) copy-start(bf16[768,768]{0,1:T(8,128)(2,1)S(1)} %convolution_convert_fusion.5) | copy-start | bytes 3538948
  401.6 11.2 %copy-start.14 = (bf16[768,12,32]{0,2,1:T(8,128)(2,1)S(1)}, bf16[768,12,32]{0,2,1:T(8,128)(2,1)}, u32[]{:S(2)}) copy-start(bf16[768,12,32]{0,2,1:T(8,128)(2,1)} %copy-done.13) | copy-start | bytes 1769476
  401.6 11.2 %copy-start.16 = (bf16[768,12,32]{0,2,1:T(8,128)(2,1)S(1)}, bf16[768,12,32]{0,2,1:T(8,128)(2,1)}, u32[]{:S(2)}) copy-start(bf16[768,12,32]{0,2,1:T(8,128)(2,1)} %copy-done.15) | copy-start | bytes 1769476
  421.9 77.4 %reduce-scatter.9.cloned.1.call-start = ((), (), s32[]{:S(2)}) async-start(), calls=%async_computation.12 | async-start | bytes 3981312 | tf_op jit(solution)/shard_map/reduce_scatter | solution.py:257
  445.2 234.6 %all-reduce.11.cloned.1.call-start = ((), (), s32[]{:S(2)}) async-start(), calls=%async_computation.20 | async-start | bytes 3538944 | tf_op jit(solution)/shard_map/psum | solution.py:278
  499.3 223.4 %reduce-scatter.23.cloned.1.call-start = ((), (), s32[]{:S(2)}) async-start(), calls=%async_computation.19 | async-start | bytes 14155776 | tf_op jit(solution)/shard_map/reduce_scatter | solution.py:188
  512.4 340.3 %reduce-scatter.19.cloned.1.call-start = ((), (), s32[]{:S(2)}) async-start(), calls=%async_computation.17 | async-start | bytes 14155776 | tf_op jit(solution)/shard_map/reduce_scatter | solution.py:182
  525.2 457.6 %reduce-scatter.21.cloned.1.call-start = ((), (), s32[]{:S(2)}) async-start(), calls=%async_computation.18 | async-start | bytes 14155776 | tf_op jit(solution)/shard_map/reduce_scatter | solution.py:185
  553.0 45.3 %all-to-all-start.1 = ((bf16[4,4,120,768]{3,2,1,0:T(8,128)(2,1)}), bf16[4,4,120,768]{3,2,1,0:T(8,128)(2,1)}, u32[]{:S(2)}, u32[]{:S(2)}) async-start(bf16[4,4,120,768]{3,2,1,0:T(8,128)(2,1)} %copy.53), calls=%async_computation.1 | async-start | bytes 5898240 | tf_op jit(solution)/shard_map/all_to_all | solution.py:144
  617.9 7.7 copy-start.39
  (26 other events, 71.4 us)
Sparse Core Ops, SparseCore 0:
  78.0 43.0 reduce-scatter.12
  144.5 42.9 reduce-scatter.14
  283.5 42.1 reduce-scatter.16
  422.0 33.0 reduce-scatter.10
  457.3 42.0 reduce-scatter.8
  503.3 87.2 all-reduce.10
  593.0 129.6 reduce-scatter.22
  725.1 127.5 reduce-scatter.18
  855.1 127.5 reduce-scatter.20
where the time goes:
time: 1000 us; the launch traced here: 993 us
  waiting for transfers between devices  405 us (40%)
  matrix products  296 us (30%)
  local copies, waits for them, and re-layouts  122 us (12%)
  other arithmetic  106 us (11%)
  blocking collectives  27.7 us (3%)
  starting transfers between devices  20 us (2%)
  between operations  16.2 us (2%)
    reduce_scatter x1, waiting for transfers between devices, shards(): lax.psum_scatter(gate_w_grad.astype(jnp.bfloat16), 'dp', scatter_dimensio...  127 us
    reduce_scatter x1, waiting for transfers between devices, shards(): lax.psum_scatter(up_w_grad.astype(jnp.bfloat16), 'dp', scatter_dimension=...  127 us
    reduce_scatter x1, waiting for transfers between devices, shards(): lax.psum_scatter(qkv_weight_grad.astype(jnp.bfloat16), 'dp', scatter_dime...  44.2 us
    all_to_all x1, waiting for transfers between devices, shards(): lax.all_to_all(expert_result, 'expert', split_axis=0, concat_axis=0, tile...  38.6 us
    reduce_scatter x1, waiting for transfers between devices, shards(): lax.psum_scatter(down_w_grad.astype(jnp.bfloat16), 'dp', scatter_dimensio...  35.5 us
    dot_general x5, matrix products, contract_last(): lax.dot_general(left_side, right_side, (((1,), (1,)), ((), ())), preferre...  34.1 us
    dot_general x5, matrix products, contract_rows(): lax.dot_general(left_side, right_side, (((0,), (0,)), ((), ())), preferre...  26.1 us
    dot_general x1, matrix products, shards(): jnp.einsum('slcd,lfd->slcf', slot_grad_in, expert_down, preferred_element...  25.5 us
  transfers between devices with their start and end apart: 13, of which 8 were waited for; matrix products, arithmetic and copies ran while one was open for 45% of the time, Pallas kernels for 0%

commit v1 on v0

--- a/solution.py
+++ b/solution.py
@@ -8,6 +8,22 @@
 E = 16
 CAP = 120
 epsilon = 1e-06
+
+
+def pairwise_exchange(x, axis, split, join):
+    ways, here = (lax.axis_size(axis), lax.axis_index(axis))
+    width = x.shape[split] // ways
+    shape = list(x.shape)
+    shape[split] = width
+    height = shape[join]
+    shape[join] = height * ways
+    full = jnp.zeros(shape, x.dtype)
+    for mask in range(ways):
+        part = lax.dynamic_slice_in_dim(x, (here ^ mask) * width, width, axis=split)
+        if mask:
+            part = lax.ppermute(part, axis, [(d, d ^ mask) for d in range(ways)])
+        full = lax.dynamic_update_slice_in_dim(full, part, (here ^ mask) * height, axis=join)
+    return full
 
 
 def rms_forward(values, gain_vector):
@@ -175,9 +191,7 @@
     dispatched_grad = dispatched_grad + jnp.einsum(
         "slcf,ldf->slcd", expert_up_back, expert_up, preferred_element_type=jnp.float32
     )
-    sent_back = lax.all_to_all(
-        dispatched_grad.astype(jnp.bfloat16), "expert", split_axis=0, concat_axis=0, tiled=True
-    )
+    sent_back = pairwise_exchange(dispatched_grad.astype(jnp.bfloat16), "expert", 0, 0)
     expert_sums = (
         lax.psum_scatter(
             gate_w_grad.astype(jnp.bfloat16), "dp", scatter_dimension=1, tiled=True

time: 1000 us -> 1050 us (1.050)
  waiting for transfers between devices: 405 us -> 445 us
    reduce_scatter x1, waiting for transfers between devices: 0.02 us -> 42.2 us  [shards(): lax.psum_scatter(shared_down_grad.astype(jnp.bfloat16), 'dp', scatter_dim...]
    all_to_all x1, waiting for transfers between devices: 38.6 us -> 0.01 us  [shards(): lax.all_to_all(expert_result, 'expert', split_axis=0, concat_axis=0, tile...]
    reduce_scatter x1, waiting for transfers between devices: 35.5 us -> 70.2 us  [shards(): lax.psum_scatter(down_w_grad.astype(jnp.bfloat16), 'dp', scatter_dimensio...]
    ppermute x0 -> x3, waiting for transfers between devices: none -> 23.9 us  [pairwise_exchange(): part = lax.ppermute(part, axis, [(d, d ^ mask) for d in range(ways)])]
    all_to_all x1 -> x0, waiting for transfers between devices: 18.2 us -> none  [shards(): lax.all_to_all(dispatched_grad.astype(jnp.bfloat16), 'expert', split_axis...]
  transfers between devices with their start and end apart: 13 -> 15, of which waited for: 8 -> 8; matrix products, arithmetic and copies ran while one was open for 45% -> 31% of each run, Pallas kernels for 0% -> 0%
where the time goes in v1:
time: 1050 us; the launch traced here: 1040 us
  waiting for transfers between devices  445 us (42%)
  matrix products  303 us (29%)
  local copies, waits for them, and re-layouts  120 us (11%)
  other arithmetic  106 us (10%)
  blocking collectives  32.9 us (3%)
  starting transfers between devices  19.3 us (2%)
  between operations  16.2 us (2%)
    reduce_scatter x1, waiting for transfers between devices, shards(): lax.psum_scatter(gate_w_grad.astype(jnp.bfloat16), 'dp', scatter_dimensio...  127 us
    reduce_scatter x1, waiting for transfers between devices, shards(): lax.psum_scatter(up_w_grad.astype(jnp.bfloat16), 'dp', scatter_dimension=...  127 us
    reduce_scatter x1, waiting for transfers between devices, shards(): lax.psum_scatter(down_w_grad.astype(jnp.bfloat16), 'dp', scatter_dimensio...  70.2 us
    reduce_scatter x1, waiting for transfers between devices, shards(): lax.psum_scatter(qkv_weight_grad.astype(jnp.bfloat16), 'dp', scatter_dime...  45.1 us
    reduce_scatter x1, waiting for transfers between devices, shards(): lax.psum_scatter(shared_down_grad.astype(jnp.bfloat16), 'dp', scatter_dim...  42.2 us
    dot_general x5, matrix products, contract_last(): lax.dot_general(left_side, right_side, (((1,), (1,)), ((), ())), preferre...  34.5 us
    dot_general x5, matrix products, contract_rows(): lax.dot_general(left_side, right_side, (((0,), (0,)), ((), ())), preferre...  26.9 us
    dot_general x1, matrix products, shards(): jnp.einsum('slcd,lfd->slcf', slot_grad_in, expert_down, preferred_element...  25.5 us
  transfers between devices with their start and end apart: 15, of which 8 were waited for; matrix products, arithmetic and copies ran while one was open for 31% of the time, Pallas kernels for 0%

profile of v1, /device:TPU:0, one launch (start us, length us, event | category | flops | bytes accessed | tf_op | source)
XLA Modules:
  0.0 1041.4 jit_solution(3688796533446629247)
XLA Ops:
  25.8 9.4 reduce-window.6
  62.1 12.0 %fusion.84 = (f32[12,768]{1,0:T(8,128)S(1)}, f32[12,768,768]{1,2,0:T(8,128)}) fusion(bf16[768,12,32]{0,2,1:T(8,128)(2,1)S(1)} %get-tuple-element.46, bf16[768,12,32]{0,2,1:T(8,128)(2,1)S(1)} %get-tuple-element.47, bf16[768,12,32]{0,2,1:T(8,128)(2,1)S(1)} %get-tuple-element.41, bf16[768,12,32]{0,2,1:T(8,128)(2,1)S(1)} %get-tuple-element.40, ...), kind=kOutput, calls=%fused_computation.169 | convolution fusion | flops 931912704 | bytes 31297536 | tf_op jit(solution)/shard_map/qhd,khd->hqk/dot_general | solution.py:128
  74.1 11.6 %fusion = f32[12,768]{1,0:T(8,128)S(1)} fusion(f32[12,768,768]{1,2,0:T(8,128)} %get-tuple-element.54, f32[12,768]{1,0:T(8,128)S(1)} %get-tuple-element.53), kind=kLoop, calls=%fused_computation.16 | loop fusion | flops 14146560 | bytes 28385280 | tf_op jit(solution)/shard_map/reduce_sum | solution.py:134
  85.7 12.3 %fusion.54 = bf16[12,64,768]{2,1,0:T(8,128)(2,1)} fusion(f32[12,768,768]{1,2,0:T(8,128)} %get-tuple-element.54, f32[12,768]{1,0:T(8,128)S(1)} %fusion, f32[12,768]{1,0:T(8,128)S(1)} %get-tuple-element.53, f32[768,3,12,64]{0,3,2,1:T(8,128)S(1)} %bitcast.180), kind=kOutput, calls=%fused_computation.100 | convolution fusion | flops 927793152 | bytes 30769152 | tf_op jit(solution)/shard_map/hqk,khd->qhd/dot_general | solution.py:137
  103.6 9.9 gather_fusion.1
  144.4 10.4 gather_fusion.3
  159.8 9.2 multiply_convert_fusion.1
  173.7 15.1 %fusion.17 = f32[4,4,120,2048]{3,2,1,0:T(8,128)} fusion(bf16[4,768,2048]{2,1,0:T(8,128)(2,1)} %param.30, bf16[4,4,120,768]{3,2,1,0:T(8,128)(2,1)} %all-to-all-done), kind=kOutput, calls=%fused_computation.38 | convolution fusion | flops 6039797760 | bytes 31260672 | tf_op jit(solution)/shard_map/slcd,ldf->slcf/dot_general | solution.py:153
  188.8 14.6 %fusion.21 = f32[4,4,120,2048]{3,2,1,0:T(8,128)} fusion(bf16[4,768,2048]{2,1,0:T(8,128)(2,1)} %param.29, bf16[4,4,120,768]{3,2,1,0:T(8,128)(2,1)} %all-to-all-done), kind=kOutput, calls=%fused_computation.42 | convolution fusion | flops 6039797760 | bytes 31260672 | tf_op jit(solution)/shard_map/slcd,ldf->slcf/dot_general | solution.py:150
  208.7 25.5 %fusion.3 = (bf16[4,4,120,2048]{3,2,0,1:T(8,128)(2,1)}, bf16[4,4,120,2048]{3,2,0,1:T(8,128)(2,1)}, bf16[4,4,120,2048]{3,2,0,1:T(8,128)(2,1)}) fusion(f32[4,4,120,2048]{3,2,1,0:T(8,128)} %fusion.17, f32[4,4,120,2048]{3,2,1,0:T(8,128)} %fusion.21, bf16[4,2048,768]{2,1,0:T(8,128)(2,1)} %param.31, bf16[4,4,120,768]{3,2,1,0:T(8,128)(2,1)} %all-to-all-done.2), kind=kOutput, calls=%fused_computation.21 | convolution fusion | flops 6098780160 | bytes 70582272 | tf_op jit(solution)/shard_map/slcd,lfd->slcf/dot_general | solution.py:175
  234.2 14.3 %fusion.15 = f32[4,4,120,768]{3,2,1,0:T(8,128)} fusion(bf16[4,4,120,2048]{3,2,0,1:T(8,128)(2,1)} %get-tuple-element.27, bf16[4,768,2048]{2,1,0:T(8,128)(2,1)} %param.30), kind=kOutput, calls=%fused_computation.36 | convolution fusion | flops 6039797760 | bytes 26345472 | tf_op jit(solution)/shard_map/slcf,ldf->slcd/dot_general | solution.py:191
  248.5 14.9 %add_convert_fusion = bf16[4,4,120,768]{3,2,1,0:T(8,128)(2,1)} fusion(f32[4,4,120,768]{3,2,1,0:T(8,128)} %fusion.15, bf16[4,4,120,2048]{3,2,0,1:T(8,128)(2,1)} %get-tuple-element.25, bf16[4,768,2048]{2,1,0:T(8,128)(2,1)} %param.29), kind=kOutput, calls=%fused_computation.55 | convolution fusion | flops 6042746880 | bytes 29294592 | tf_op jit(solution)/shard_map/slcf,ldf->slcd/dot_general | solution.py:188
  277.4 23.9 %collective-permute-done = bf16[1,4,120,768]{3,2,1,0:T(8,128)(2,1)} collective-permute-done((bf16[1,4,120,768]{3,2,1,0:T(8,128)(2,1)}, bf16[1,4,120,768]{3,2,1,0:T(8,128)(2,1)}, u32[]{:S(2)}, u32[]{:S(2)}) %collective-permute-start) | collective-permute-done | bytes 737312 | tf_op jit(solution)/shard_map/ppermute | solution.py:24
  306.7 9.0 gather_fusion.4
  322.1 9.4 reduce_sum.104
  368.9 23.6 %multiply_reduce_fusion = (f32[12,768]{1,0:T(8,128)}, f32[12,768,768]{1,2,0:T(8,128)}) fusion(f32[12,768,768]{1,2,0:T(8,128)} %get-tuple-element.54, f32[12,768]{1,0:T(8,128)S(1)} %log_add_fusion, bf16[768,12,64]{0,2,1:T(8,128)(2,1)S(1)} %bitcast.182, f32[768,3,12,64]{0,3,2,1:T(8,128)} %bitcast.181), kind=kOutput, calls=%fused_computation.8 | convolution fusion | flops 927194112 | bytes 59056128 | tf_op jit(solution)/shard_map/qhd,khd->hqk/dot_general | solution.py:241
  392.4 24.1 %multiply_convert_fusion = bf16[12,768,768]{1,2,0:T(8,128)(2,1)} fusion(f32[12,768,768]{1,2,0:T(8,128)} %get-tuple-element.59, f32[12,768,768]{1,2,0:T(8,128)} %get-tuple-element.54, f32[12,768]{1,0:T(8,128)} %get-tuple-element.58, f32[12,768]{1,0:T(8,128)} %copy-done.20), kind=kLoop, calls=%fused_computation.7 | loop fusion | flops 28311552 | bytes 70852608 | tf_op jit(solution)/shard_map/convert_element_type | solution.py:245
  416.5 9.9 multiply_bitcast_fusion
  436.4 11.9 %fusion.55 = bf16[768,1,12,64]{0,3,2,1:T(8,128)(2,1)S(1)} fusion(bf16[768,12,64]{0,2,1:T(8,128)(2,1)S(1)} %bitcast.183, f32[12,768,768]{1,2,0:T(8,128)} %get-tuple-element.54, f32[12,768]{1,0:T(8,128)S(1)} %copy-done.21), kind=kOutput, calls=%fused_computation.101 | convolution fusion | flops 920715264 | bytes 30707712 | tf_op jit(solution)/shard_map/hqk,qhd->khd/dot_general | solution.py:235
  460.6 42.2 %reduce-scatter.17.cloned.1.call-done = bf16[256,768]{1,0:T(8,128)(2,1)} async-done(((bf16[2048,768]{1,0:T(8,128)(2,1)}), bf16[256,768]{1,0:T(8,128)(2,1)}) %reduce-scatter.17.cloned.1.call-update) | async-done | bytes 393232 | tf_op jit(solution)/shard_map/reduce_scatter | solution.py:286
  502.8 45.1 %reduce-scatter.9.cloned.1.call-done = bf16[96,2304]{1,0:T(8,128)(2,1)} async-done(((bf16[768,2304]{1,0:T(8,128)(2,1)}), bf16[96,2304]{1,0:T(8,128)(2,1)}) %reduce-scatter.9.cloned.1.call-update) | async-done | bytes 442384 | tf_op jit(solution)/shard_map/reduce_scatter | solution.py:271
  548.0 12.9 %bitcast_convert_fusion = bf16[4,2048,768]{2,1,0:T(8,128)(2,1)} fusion(bf16[4,4,120,2048]{3,2,0,1:T(8,128)(2,1)} %get-tuple-element.26, bf16[4,4,120,768]{3,2,1,0:T(8,128)(2,1)} %all-to-all-done.2), kind=kOutput, calls=%fused_computation.13 | convolution fusion | flops 6046089216 | bytes 23396352 | tf_op jit(solution)/shard_map/slcf,slcd->lfd/dot_general | solution.py:172
  560.9 12.7 %bitcast_convert_fusion.2 = bf16[4,768,2048]{2,1,0:T(8,128)(2,1)} fusion(bf16[4,4,120,768]{3,2,1,0:T(8,128)(2,1)} %all-to-all-done, bf16[4,4,120,2048]{3,2,0,1:T(8,128)(2,1)} %get-tuple-element.25), kind=kOutput, calls=%fused_computation.15 | convolution fusion | flops 6046089216 | bytes 23396352 | tf_op jit(solution)/shard_map/slcd,slcf->ldf/dot_general | solution.py:182
  573.7 13.2 %bitcast_convert_fusion.1 = bf16[4,768,2048]{2,1,0:T(8,128)(2,1)} fusion(bf16[4,4,120,768]{3,2,1,0:T(8,128)(2,1)} %all-to-all-done, bf16[4,4,120,2048]{3,2,0,1:T(8,128)(2,1)} %get-tuple-element.27), kind=kOutput, calls=%fused_computation.14 | convolution fusion | flops 6046089216 | bytes 23396352 | tf_op jit(solution)/shard_map/slcd,slcf->ldf/dot_general | solution.py:185
  587.0 12.7 %convert_bitcast_fusion = bf16[4,4,120,768]{3,2,0,1:T(8,128)(2,1)S(1)} fusion(bf16[4,4,120,2048]{3,2,0,1:T(8,128)(2,1)} %get-tuple-element.26, bf16[4,2048,768]{2,1,0:T(8,128)(2,1)} %param.31), kind=kOutput, calls=%fused_computation.69 | convolution fusion | flops 6041272320 | bytes 23396352 | tf_op jit(solution)/shard_map/slcf,lfd->slcd/dot_general | solution.py:157
  615.3 15.2 %all-reduce.6 = (bf16[768]{0:T(1024)(128)(2,1)}, bf16[768]{0:T(1024)(128)(2,1)}) all-reduce(bf16[768]{0:T(1024)(128)(2,1)} %get-tuple-element.14, bf16[768]{0:T(1024)(128)(2,1)S(1)} %copy-done.40), channel_id=2, replica_groups=mesh['dp'=8,'expert'=4] {'dp'}, use_global_device_ids=true, to_apply=%region_15.16.clone | all-reduce | flops 1536 | bytes 6144
  632.5 17.8 %all-reduce.7 = (bf16[96]{0:T(256)(128)(2,1)}, bf16[96]{0:T(256)(128)(2,1)}) all-reduce(bf16[96]{0:T(256)(128)(2,1)S(1)} %dynamic-slice.17, bf16[96]{0:T(256)(128)(2,1)} %dynamic-slice.19), channel_id=1, replica_groups=mesh['dp'=8,'expert'=4] {'expert'}, use_global_device_ids=true, to_apply=%region_16.17 | all-reduce | flops 192 | bytes 768 | tf_op jit(solution)/shard_map/psum | solution.py:291
  660.7 9.0 gather_fusion.2
  676.0 9.6 multiply_reduce_fusion.1
  701.1 70.2 %reduce-scatter.23.cloned.1.call-done = bf16[4,256,768]{2,1,0:T(8,128)(2,1)} async-done(((bf16[4,2048,768]{2,1,0:T(8,128)(2,1)}), bf16[4,256,768]{2,1,0:T(8,128)(2,1)}) %reduce-scatter.23.cloned.1.call-update) | async-done | bytes 1572880 | tf_op jit(solution)/shard_map/reduce_scatter | solution.py:202
  774.6 126.7 %reduce-scatter.19.cloned.1.call-done = bf16[4,96,2048]{2,1,0:T(8,128)(2,1)} async-done(((bf16[4,768,2048]{2,1,0:T(8,128)(2,1)}), bf16[4,96,2048]{2,1,0:T(8,128)(2,1)}) %reduce-scatter.19.cloned.1.call-update) | async-done | bytes 1572880 | tf_op jit(solution)/shard_map/reduce_scatter | solution.py:196
  904.7 126.6 %reduce-scatter.21.cloned.1.call-done = bf16[4,96,2048]{2,1,0:T(8,128)(2,1)} async-done(((bf16[4,768,2048]{2,1,0:T(8,128)(2,1)}), bf16[4,96,2048]{2,1,0:T(8,128)(2,1)}) %reduce-scatter.21.cloned.1.call-update) | async-done | bytes 1572880 | tf_op jit(solution)/shard_map/reduce_scatter | solution.py:199
  (205 shorter events, 240.5 us)
Async XLA Ops:
  7.2 48.6 %copy-start = (bf16[768,2304]{1,0:T(8,128)(2,1)S(1)}, bf16[768,2304]{1,0:T(8,128)(2,1)}, u32[]{:S(2)}) copy-start(bf16[768,2304]{1,0:T(8,128)(2,1)} %param.23) | copy-start | bytes 10616836
  47.9 12.3 %copy-start.32 = (s32[1536]{0:T(1024)}, s32[1536]{0:T(1024)S(1)}, u32[]{:S(2)}) copy-start(s32[1536]{0:T(1024)S(1)} %compare_select_fusion.2) | copy-start | bytes 18436
  60.2 25.5 %copy-start.4 = (f32[768,2304]{0,1:T(8,128)}, f32[768,2304]{0,1:T(8,128)S(1)}, u32[]{:S(2)}) copy-start(f32[768,2304]{0,1:T(8,128)S(1)} %fusion.65) | copy-start | bytes 21233668
  62.1 12.0 %copy-start.13 = (bf16[768,12,32]{0,2,1:T(8,128)(2,1)}, bf16[768,12,32]{0,2,1:T(8,128)(2,1)S(1)}, u32[]{:S(2)}) copy-start(bf16[768,12,32]{0,2,1:T(8,128)(2,1)S(1)} %get-tuple-element.46) | copy-start | bytes 1769476
  62.1 12.0 %copy-start.15 = (bf16[768,12,32]{0,2,1:T(8,128)(2,1)}, bf16[768,12,32]{0,2,1:T(8,128)(2,1)S(1)}, u32[]{:S(2)}) copy-start(bf16[768,12,32]{0,2,1:T(8,128)(2,1)S(1)} %get-tuple-element.47) | copy-start | bytes 1769476
  62.1 12.0 %copy-start.16 = (bf16[768,12,32]{0,2,1:T(8,128)(2,1)}, bf16[768,12,32]{0,2,1:T(8,128)(2,1)S(1)}, u32[]{:S(2)}) copy-start(bf16[768,12,32]{0,2,1:T(8,128)(2,1)S(1)} %get-tuple-element.40) | copy-start | bytes 1769476
  62.1 12.0 %copy-start.17 = (bf16[768,12,32]{0,2,1:T(8,128)(2,1)}, bf16[768,12,32]{0,2,1:T(8,128)(2,1)S(1)}, u32[]{:S(2)}) copy-start(bf16[768,12,32]{0,2,1:T(8,128)(2,1)S(1)} %get-tuple-element.41) | copy-start | bytes 1769476
  74.1 11.6 %copy-start.26 = (f32[12,768]{1,0:T(8,128)}, f32[12,768]{1,0:T(8,128)S(1)}, u32[]{:S(2)}) copy-start(f32[12,768]{1,0:T(8,128)S(1)} %get-tuple-element.53) | copy-start | bytes 110596
  85.7 12.3 %copy-start.27 = (f32[12,768]{1,0:T(8,128)}, f32[12,768]{1,0:T(8,128)S(1)}, u32[]{:S(2)}) copy-start(f32[12,768]{1,0:T(8,128)S(1)} %fusion) | copy-start | bytes 110596
  85.7 12.3 %copy-start.8 = (bf16[768,768]{1,0:T(8,128)(2,1)S(1)}, bf16[768,768]{1,0:T(8,128)(2,1)}, u32[]{:S(2)}) copy-start(bf16[768,768]{1,0:T(8,128)(2,1)} %param.16) | copy-start | bytes 3538948
  113.5 55.5 %all-to-all-start = ((bf16[4,4,120,768]{3,2,1,0:T(8,128)(2,1)}), bf16[4,4,120,768]{3,2,1,0:T(8,128)(2,1)}, u32[]{:S(2)}, u32[]{:S(2)}) async-start(bf16[4,4,120,768]{3,2,1,0:T(8,128)(2,1)} %bitcast.176), calls=%async_computation | async-start | bytes 5898240 | tf_op jit(solution)/shard_map/all_to_all | solution.py:149
  169.0 39.7 %all-to-all-start.2 = ((bf16[4,4,120,768]{3,2,1,0:T(8,128)(2,1)}), bf16[4,4,120,768]{3,2,1,0:T(8,128)(2,1)}, u32[]{:S(2)}, u32[]{:S(2)}) async-start(bf16[4,4,120,768]{3,2,1,0:T(8,128)(2,1)} %bitcast.177), calls=%async_computation.2 | async-start | bytes 5898240 | tf_op jit(solution)/shard_map/all_to_all | solution.py:171
  173.6 281.9 %reduce-scatter.11.cloned.1.call-start = ((), (), s32[]{:S(2)}) async-start(), calls=%async_computation.12 | async-start | bytes 1327104 | tf_op jit(solution)/shard_map/reduce_scatter | solution.py:274
  266.5 37.1 %collective-permute-start.2 = (bf16[1,4,120,768]{3,2,1,0:T(8,128)(2,1)}, bf16[1,4,120,768]{3,2,1,0:T(8,128)(2,1)}, u32[]{:S(2)}, u32[]{:S(2)}) collective-permute-start(bf16[1,4,120,768]{3,2,1,0:T(8,128)(2,1)} %get-tuple-element.33), channel_id=1, source_target_pairs={{0,3},{1,2},{2,1},{3,0},{4,7},{5,6},{6,5},{7,4},{8,11},{9,10},{10,... | collective-permute-start | bytes 2211848 | tf_op jit(solution)/shard_map/ppermute | solution.py:24
  268.0 34.5 %collective-permute-start.1 = (bf16[1,4,120,768]{3,2,1,0:T(8,128)(2,1)}, bf16[1,4,120,768]{3,2,1,0:T(8,128)(2,1)}, u32[]{:S(2)}, u32[]{:S(2)}) collective-permute-start(bf16[1,4,120,768]{3,2,1,0:T(8,128)(2,1)} %get-tuple-element.34), channel_id=1, source_target_pairs={{0,2},{1,3},{2,0},{3,1},{4,6},{5,7},{6,4},{7,5},{8,10},{9,11},{10,... | collective-permute-start | bytes 2211848 | tf_op jit(solution)/shard_map/ppermute | solution.py:24
  269.5 31.8 %collective-permute-start = (bf16[1,4,120,768]{3,2,1,0:T(8,128)(2,1)}, bf16[1,4,120,768]{3,2,1,0:T(8,128)(2,1)}, u32[]{:S(2)}, u32[]{:S(2)}) collective-permute-start(bf16[1,4,120,768]{3,2,1,0:T(8,128)(2,1)} %get-tuple-element.35), channel_id=1, source_target_pairs={{0,1},{1,0},{2,3},{3,2},{4,5},{5,4},{6,7},{7,6},{8,9},{9,8},{10,11... | collective-permute-start | bytes 2211848 | tf_op jit(solution)/shard_map/ppermute | solution.py:24
  276.0 30.7 %copy-start.28 = (s32[2048]{0:T(1024)}, s32[2048]{0:T(1024)S(1)}, u32[]{:S(2)}) copy-start(s32[2048]{0:T(1024)S(1)} %pad_clamp_fusion.1) | copy-start | bytes 24580
  322.0 9.4 copy-start.31
  322.0 9.4 copy-start.36
  331.4 8.7 copy-start.2
  331.4 8.7 copy-start.6
  344.3 111.2 %reduce-scatter.13.cloned.1.call-start = ((), (), s32[]{:S(2)}) async-start(), calls=%async_computation.13 | async-start | bytes 3538944 | tf_op jit(solution)/shard_map/reduce_scatter | solution.py:280
  351.5 109.0 %reduce-scatter.15.cloned.1.call-start = ((), (), s32[]{:S(2)}) async-start(), calls=%async_computation.14 | async-start | bytes 3538944 | tf_op jit(solution)/shard_map/reduce_scatter | solution.py:283
  358.2 144.6 %reduce-scatter.17.cloned.1.call-start = ((), (), s32[]{:S(2)}) async-start(), calls=%async_computation.15 | async-start | bytes 3538944 | tf_op jit(solution)/shard_map/reduce_scatter | solution.py:286
  364.8 183.1 %reduce-scatter.9.cloned.1.call-start = ((), (), s32[]{:S(2)}) async-start(), calls=%async_computation.11 | async-start | bytes 3981312 | tf_op jit(solution)/shard_map/reduce_scatter | solution.py:271
  368.8 23.6 %copy-start.10 = (bf16[768,768]{0,1:T(8,128)(2,1)}, bf16[768,768]{0,1:T(8,128)(2,1)S(1)}, u32[]{:S(2)}) copy-start(bf16[768,768]{0,1:T(8,128)(2,1)S(1)} %convolution_convert_fusion.5) | copy-start | bytes 3538948
  416.5 9.9 copy-start.14
  455.5 238.1 %all-reduce.11.cloned.1.call-start = ((), (), s32[]{:S(2)}) async-start(), calls=%async_computation.19 | async-start | bytes 3538944 | tf_op jit(solution)/shard_map/psum | solution.py:292
  547.9 223.3 %reduce-scatter.23.cloned.1.call-start = ((), (), s32[]{:S(2)}) async-start(), calls=%async_computation.18 | async-start | bytes 14155776 | tf_op jit(solution)/shard_map/reduce_scatter | solution.py:202
  560.9 340.4 %reduce-scatter.19.cloned.1.call-start = ((), (), s32[]{:S(2)}) async-start(), calls=%async_computation.16 | async-start | bytes 14155776 | tf_op jit(solution)/shard_map/reduce_scatter | solution.py:196
  573.7 457.6 %reduce-scatter.21.cloned.1.call-start = ((), (), s32[]{:S(2)}) async-start(), calls=%async_computation.17 | async-start | bytes 14155776 | tf_op jit(solution)/shard_map/reduce_scatter | solution.py:199
  601.5 55.5 %all-to-all-start.1 = ((bf16[4,4,120,768]{3,2,1,0:T(8,128)(2,1)}), bf16[4,4,120,768]{3,2,1,0:T(8,128)(2,1)}, u32[]{:S(2)}, u32[]{:S(2)}) async-start(bf16[4,4,120,768]{3,2,1,0:T(8,128)(2,1)} %copy.52), calls=%async_computation.1 | async-start | bytes 5898240 | tf_op jit(solution)/shard_map/all_to_all | solution.py:160
  (28 other events, 102.2 us)
Sparse Core Ops, SparseCore 0:
  344.4 32.7 reduce-scatter.10
  379.6 38.5 reduce-scatter.12
  421.1 39.4 reduce-scatter.14
  463.3 39.4 reduce-scatter.16
  505.0 42.9 reduce-scatter.8
  551.9 87.5 all-reduce.10
  641.9 129.3 reduce-scatter.22
  773.6 127.5 reduce-scatter.18
  903.7 127.5 reduce-scatter.20
